TPU v7x, 32 devices: a whole 2x2x4 slice. The times are simulated.
32 devices in a mesh: gx: 8 (over y, x, core), gy: 4 (over z).
Axes of the slice: x: 2, y: 2, z: 4, core: 2. Of those that a mesh axis runs over, the one named last changes fastest.
Arguments:
- candidate_owner: int32 [256, 512, 1], P(('gx', 'gy')), may hold values from 0 to 31; in each aligned block of 4096 rows (0 to 4095, 4096 to 8191, ..., all dimensions but the last counted through in order) at most 256 rows name the same one
- candidate_row: int32 [256, 512], P(('gx', 'gy')), may hold values from 0 to 78335
- item_table: bfloat16 [2506752, 128], P(('gx', 'gy')), may hold values from -6 to 6
- w_in: bfloat16 [128, 512], replicated, may hold values from -0.5 to 0.5
- w_qkv: bfloat16 [1, 512, 1536], replicated, may hold values from -0.25 to 0.25
- w_out: bfloat16 [1, 512, 512], replicated, may hold values from -0.25 to 0.25
- w_up: bfloat16 [1, 512, 1024], replicated, may hold values from -0.25 to 0.25
- w_down: bfloat16 [1, 1024, 512], replicated, may hold values from -0.1875 to 0.1875
- norm_gains: float32 [1, 2, 512], replicated, may hold values from 0.25 to 1.75
- final_gain: float32 [512], replicated, may hold values from 0.25 to 1.75
- w_score: bfloat16 [512], replicated, may hold values from -0.25 to 0.25
Outputs:
- log_probs: float32 [256, 512], P(('gx', 'gy'))
Inputs may be any that keep to these rules, and one draw needn't show every extreme that they name: `candidate_owner`: among the candidates of one device's 8 slates no shard is named more than 256 times, a bound that some block reaches.
All inputs are finite; a program needn't handle non-finite values.
Results may differ from a plain program's by a relative error of at most 0.0007.
Values may be sent and summed in bfloat16 or wider, within the bound.
No kernel may reach another device: no remote copies, remote signals or barrier semaphores. Data moves between devices by JAX's collectives and lax.ppermute only.
A program may use at most 128 MiB of HBM per device.

v0:
```python
import jax
import jax.numpy as jnp
from jax import lax
from jax.sharding import PartitionSpec as P

HEADS = 8


def layer_norm(values, gain):
    mean = jnp.mean(values, axis=-1, keepdims=True)
    centred = values - mean
    variance = jnp.mean(centred * centred, axis=-1, keepdims=True)
    return centred * lax.rsqrt(variance + 1e-05) * gain


def attend_slate(operands):
    query, keys, values = operands
    length = query.shape[0]
    head_dim = query.shape[-1]
    scores = jnp.einsum(
        "qhd,khd->hqk", query, keys, preferred_element_type=jnp.float32
    ) * head_dim ** (-0.5)
    probs = jax.nn.softmax(scores, axis=-1).astype(jnp.bfloat16)
    mixed = jnp.einsum("hqk,khd->qhd", probs, values, preferred_element_type=jnp.float32)
    return mixed.astype(jnp.bfloat16).reshape(length, HEADS * head_dim)


def score_slates(emb, w_in, w_qkv, w_out, w_up, w_down, norm_gains, final_gain, w_score):
    slates, length, width = emb.shape
    model = w_in.shape[1]
    head_dim = model // HEADS
    resid = jnp.dot(emb.reshape(slates * length, width), w_in, preferred_element_type=jnp.float32)
    normed = layer_norm(resid, norm_gains[0, 0]).astype(jnp.bfloat16)
    weights = w_qkv[0]
    query = jnp.dot(normed, weights[:, :model], preferred_element_type=jnp.float32).astype(
        jnp.bfloat16
    )
    keys = jnp.dot(
        normed, weights[:, model : 2 * model], preferred_element_type=jnp.float32
    ).astype(jnp.bfloat16)
    values = jnp.dot(normed, weights[:, 2 * model :], preferred_element_type=jnp.float32).astype(
        jnp.bfloat16
    )
    query = query.reshape(slates, length, HEADS, head_dim)
    keys = keys.reshape(slates, length, HEADS, head_dim)
    values = values.reshape(slates, length, HEADS, head_dim)
    mixed = lax.map(attend_slate, (query, keys, values)).reshape(slates * length, model)
    resid = resid + jnp.dot(mixed, w_out[0], preferred_element_type=jnp.float32)
    normed = layer_norm(resid, norm_gains[0, 1]).astype(jnp.bfloat16)
    inner = jax.nn.gelu(jnp.dot(normed, w_up[0], preferred_element_type=jnp.float32)).astype(
        jnp.bfloat16
    )
    resid = resid + jnp.dot(inner, w_down[0], preferred_element_type=jnp.float32)
    final = layer_norm(resid, final_gain)
    logits = jnp.sum(final * w_score.astype(jnp.float32)[None, :], axis=-1)
    return jax.nn.log_softmax(logits.reshape(slates, length), axis=-1)


def slot_numbers(owner, shards, length):
    total = owner.shape[0]
    onehot = (owner[:, None] == jnp.arange(shards, dtype=jnp.int32)[None, :]).astype(jnp.bfloat16)
    blocks = onehot.reshape(total // length, length, shards)
    lower = (jnp.arange(length)[:, None] >= jnp.arange(length)[None, :]).astype(jnp.bfloat16)
    within = jnp.einsum("ij,bjn->bin", lower, blocks, preferred_element_type=jnp.float32)
    totals = within[:, -1, :]
    before = jnp.cumsum(totals, axis=0) - totals
    counts = within + before[:, None, :]
    picked = jnp.sum(counts * blocks.astype(jnp.float32), axis=-1)
    return (picked.reshape(total) - 1.0).astype(jnp.int32)


def fetch_rows(item_table, wanted):
    flat = wanted.reshape(-1)
    rows = jnp.take(item_table, jnp.maximum(flat, 0), axis=0)
    rows = jnp.where((flat >= 0)[:, None], rows, jnp.zeros_like(rows))
    return rows.reshape(wanted.shape + (item_table.shape[1],))


def per_device(
    candidate_owner,
    candidate_row,
    item_table,
    w_in,
    w_qkv,
    w_out,
    w_up,
    w_down,
    norm_gains,
    final_gain,
    w_score,
):
    slates, length, unused = candidate_owner.shape
    width = item_table.shape[1]
    shards = lax.axis_size(("gx", "gy"))
    capacity = max(2, 2 * slates * length // shards)
    owner = candidate_owner.reshape(slates * length)
    row_index = candidate_row.reshape(slates * length)
    slot = slot_numbers(owner, shards, length)
    position = owner * capacity + slot
    outgoing = jnp.full((shards * capacity,), -1, jnp.int32).at[position].set(row_index)
    outgoing = outgoing.reshape(shards, capacity)
    found = fetch_rows(
        item_table, lax.all_to_all(outgoing, ("gx", "gy"), split_axis=0, concat_axis=0, tiled=True)
    )
    returned = lax.all_to_all(found, ("gx", "gy"), split_axis=0, concat_axis=0, tiled=True)
    returned = returned.reshape(shards * capacity, width)
    emb = jnp.take(returned, position, axis=0).reshape(slates, length, width)
    return score_slates(emb, w_in, w_qkv, w_out, w_up, w_down, norm_gains, final_gain, w_score)


def solution(mesh):
    return jax.shard_map(
        per_device,
        mesh=mesh,
        in_specs=(
            P(("gx", "gy"), None, None),
            P(("gx", "gy"), None),
            P(("gx", "gy"), None),
            P(),
            P(),
            P(),
            P(),
            P(),
            P(),
            P(),
            P(),
        ),
        out_specs=P(("gx", "gy"), None),
        check_vma=False,
    )
```

profile of v0, /device:TPU:1, one launch (start us, length us, event | category | flops | bytes accessed | tf_op | source)
XLA Modules:
  0.0 355.7 jit_solution(8072462239938948020)
XLA Ops:
  3.1 15.5 %scatter_custom_fusion = s32[8192]{0:T(1024)S(1)} fusion(s32[4096]{0:T(1024)S(1)} %bitcast.103, s32[4096]{0:T(1024)S(1)} %bitcast.110, s32[]{:T(128)} %constant.82.clone.1), kind=kCustom, calls=%fused_computation.85 | custom fusion | bytes 32772 | tf_op jit(solution)/shard_map/scatter | solution.py:100
  18.7 13.7 %all_to_all.14 = s32[32,1,256]{2,1,0:T(1,128)S(1)} all-to-all(s32[32,1,256]{2,1,0:T(1,128)S(1)} %bitcast.101), channel_id=1, replica_groups=mesh['gx'=8,'gy'=4] {'gx','gy'}, dimensions={0} | all-to-all | bytes 65536 | tf_op jit(solution)/shard_map/all_to_all | solution.py:103
  32.4 31.1 %gather_fusion = bf16[8192,128]{1,0:T(8,128)(2,1)S(1)} fusion(bf16[78336,128]{1,0:T(8,128)(2,1)} %param.15, s32[8192]{0:T(1024)S(1)} %broadcast_clamp_fusion), kind=kCustom, calls=%fused_computation | custom fusion | bytes 4227072 | tf_op jit(solution)/shard_map/jit(_take)/gather | solution.py:74
  63.6 4.6 %select_select_fusion = bf16[32,256,128]{2,1,0:T(8,128)(2,1)} fusion(bf16[32,256,128]{2,1,0:T(8,128)(2,1)S(1)} %bitcast.98, pred[32,256]{1,0:T(8,128)(4,1)S(1)} %get-tuple-element.66, pred[32,256]{1,0:T(8,128)(4,1)S(1)} %get-tuple-element.65), kind=kLoop, calls=%fused_computation.53 | loop fusion | flops 2097152 | bytes 4210688 | tf_op jit(solution)/shard_map/jit(_where)/select_n | solution.py:75
  71.9 47.8 %all-to-all-done.1 = bf16[32,256,128]{2,1,0:T(8,128)(2,1)S(1)} async-done(((bf16[32,256,128]{2,1,0:T(8,128)(2,1)}), bf16[32,256,128]{2,1,0:T(8,128)(2,1)S(1)}, u32[]{:S(2)}, u32[]{:S(2)}) %all-to-all-start.1) | async-done | bytes 2097184 | tf_op jit(solution)/shard_map/all_to_all | solution.py:105
  119.7 14.9 %gather_fusion.1 = bf16[4096,128]{1,0:T(8,128)(2,1)} fusion(bf16[8192,128]{1,0:T(8,128)(2,1)S(1)} %bitcast.95, s32[4096]{0:T(1024)S(1)} %broadcast_clamp_fusion.1), kind=kCustom, calls=%fused_computation.1 | custom fusion | bytes 2113536 | tf_op jit(solution)/shard_map/jit(_take)/gather | solution.py:107
  155.2 11.2 %reshape.228 = bf16[8,512,8,64]{3,2,1,0:T(8,128)(2,1)} reshape(bf16[4096,512]{1,0:T(8,128)(2,1)} %convolution_convert_fusion.2) | data formatting | bytes 8388608 | tf_op jit(solution)/shard_map/reshape | solution.py:46
  166.4 9.8 %copy.38 = bf16[8,512,8,64]{1,3,2,0:T(8,128)(2,1)} copy(bf16[8,512,8,64]{3,2,1,0:T(8,128)(2,1)} %reshape.228) | data formatting | bytes 8388608 | tf_op jit(solution)/shard_map/while | solution.py:47
  176.1 11.2 %reshape.229 = bf16[8,512,8,64]{3,2,1,0:T(8,128)(2,1)} reshape(bf16[4096,512]{1,0:T(8,128)(2,1)} %convolution_convert_fusion.1) | data formatting | bytes 8388608 | tf_op jit(solution)/shard_map/reshape | solution.py:44
  187.3 9.7 %copy.39 = bf16[8,512,8,64]{1,3,2,0:T(8,128)(2,1)} copy(bf16[8,512,8,64]{3,2,1,0:T(8,128)(2,1)} %reshape.229) | data formatting | bytes 8388608 | tf_op jit(solution)/shard_map/while | solution.py:47
  197.1 11.2 %reshape.230 = bf16[8,512,8,64]{3,2,1,0:T(8,128)(2,1)} reshape(bf16[4096,512]{1,0:T(8,128)(2,1)} %convolution_convert_fusion) | data formatting | bytes 8388608 | tf_op jit(solution)/shard_map/reshape | solution.py:45
  208.3 9.7 %copy.40 = bf16[8,512,8,64]{1,3,2,0:T(8,128)(2,1)} copy(bf16[8,512,8,64]{3,2,1,0:T(8,128)(2,1)} %reshape.230) | data formatting | bytes 8388608 | tf_op jit(solution)/shard_map/while | solution.py:47
  218.0 101.8 %while.10 = (s32[]{:T(128)}, bf16[8,512,512]{2,1,0:T(8,128)(2,1)}, bf16[8,512,8,64]{1,3,2,0:T(8,128)(2,1)}, bf16[8,512,8,64]{1,3,2,0:T(8,128)(2,1)}, bf16[8,512,8,64]{1,3,2,0:T(8,128)(2,1)}, /*index=5*/s32[]{:T(128)}) while((s32[]{:T(128)}, bf16[8,512,512]{2,1,0:T(8,128)(2,1)}, bf16[8,512,8,64]{1,3,2,0:T(8,128)(2,1)}, ...), condition=%wide.region_8.9_spmd, body=%wide.region_5.8_spmd.sunk | while | flops 547619328 | bytes 21006404 | solution.py:47
  218.0 7.3 %fusion.110 = (f32[8,512]{1,0:T(8,128)S(1)}, f32[8,512,512]{1,2,0:T(8,128)}) fusion(bf16[8,512,8,64]{1,3,2,0:T(8,128)(2,1)} %get-tuple-element.128, s32[]{:T(128)} %get-tuple-element.118, bf16[8,512,8,64]{1,3,2,0:T(8,128)(2,1)} %get-tuple-element.127), kind=kOutput, calls=%fused_computation.101.clone.1 | convolution fusion | flops 274727424 | bytes 9454592 | tf_op jit(solution)/shard_map/while/body/eval_jaxpr/sub | solution.py:23
  230.8 7.2 %fusion.110 = (f32[8,512]{1,0:T(8,128)S(1)}, f32[8,512,512]{1,2,0:T(8,128)}) fusion(bf16[8,512,8,64]{1,3,2,0:T(8,128)(2,1)} %get-tuple-element.128, s32[]{:T(128)} %get-tuple-element.118, bf16[8,512,8,64]{1,3,2,0:T(8,128)(2,1)} %get-tuple-element.127), kind=kOutput, calls=%fused_computation.101.clone.1 | convolution fusion | flops 274727424 | bytes 9454592 | tf_op jit(solution)/shard_map/while/body/eval_jaxpr/sub | solution.py:23
  243.6 7.2 %fusion.110 = (f32[8,512]{1,0:T(8,128)S(1)}, f32[8,512,512]{1,2,0:T(8,128)}) fusion(bf16[8,512,8,64]{1,3,2,0:T(8,128)(2,1)} %get-tuple-element.128, s32[]{:T(128)} %get-tuple-element.118, bf16[8,512,8,64]{1,3,2,0:T(8,128)(2,1)} %get-tuple-element.127), kind=kOutput, calls=%fused_computation.101.clone.1 | convolution fusion | flops 274727424 | bytes 9454592 | tf_op jit(solution)/shard_map/while/body/eval_jaxpr/sub | solution.py:23
  256.3 7.2 %fusion.110 = (f32[8,512]{1,0:T(8,128)S(1)}, f32[8,512,512]{1,2,0:T(8,128)}) fusion(bf16[8,512,8,64]{1,3,2,0:T(8,128)(2,1)} %get-tuple-element.128, s32[]{:T(128)} %get-tuple-element.118, bf16[8,512,8,64]{1,3,2,0:T(8,128)(2,1)} %get-tuple-element.127), kind=kOutput, calls=%fused_computation.101.clone.1 | convolution fusion | flops 274727424 | bytes 9454592 | tf_op jit(solution)/shard_map/while/body/eval_jaxpr/sub | solution.py:23
  269.0 7.2 %fusion.110 = (f32[8,512]{1,0:T(8,128)S(1)}, f32[8,512,512]{1,2,0:T(8,128)}) fusion(bf16[8,512,8,64]{1,3,2,0:T(8,128)(2,1)} %get-tuple-element.128, s32[]{:T(128)} %get-tuple-element.118, bf16[8,512,8,64]{1,3,2,0:T(8,128)(2,1)} %get-tuple-element.127), kind=kOutput, calls=%fused_computation.101.clone.1 | convolution fusion | flops 274727424 | bytes 9454592 | tf_op jit(solution)/shard_map/while/body/eval_jaxpr/sub | solution.py:23
  281.7 7.2 %fusion.110 = (f32[8,512]{1,0:T(8,128)S(1)}, f32[8,512,512]{1,2,0:T(8,128)}) fusion(bf16[8,512,8,64]{1,3,2,0:T(8,128)(2,1)} %get-tuple-element.128, s32[]{:T(128)} %get-tuple-element.118, bf16[8,512,8,64]{1,3,2,0:T(8,128)(2,1)} %get-tuple-element.127), kind=kOutput, calls=%fused_computation.101.clone.1 | convolution fusion | flops 274727424 | bytes 9454592 | tf_op jit(solution)/shard_map/while/body/eval_jaxpr/sub | solution.py:23
  294.4 7.2 %fusion.110 = (f32[8,512]{1,0:T(8,128)S(1)}, f32[8,512,512]{1,2,0:T(8,128)}) fusion(bf16[8,512,8,64]{1,3,2,0:T(8,128)(2,1)} %get-tuple-element.128, s32[]{:T(128)} %get-tuple-element.118, bf16[8,512,8,64]{1,3,2,0:T(8,128)(2,1)} %get-tuple-element.127), kind=kOutput, calls=%fused_computation.101.clone.1 | convolution fusion | flops 274727424 | bytes 9454592 | tf_op jit(solution)/shard_map/while/body/eval_jaxpr/sub | solution.py:23
  307.1 7.2 %fusion.110 = (f32[8,512]{1,0:T(8,128)S(1)}, f32[8,512,512]{1,2,0:T(8,128)}) fusion(bf16[8,512,8,64]{1,3,2,0:T(8,128)(2,1)} %get-tuple-element.128, s32[]{:T(128)} %get-tuple-element.118, bf16[8,512,8,64]{1,3,2,0:T(8,128)(2,1)} %get-tuple-element.127), kind=kOutput, calls=%fused_computation.101.clone.1 | convolution fusion | flops 274727424 | bytes 9454592 | tf_op jit(solution)/shard_map/while/body/eval_jaxpr/sub | solution.py:23
  319.8 7.1 %fusion.93 = (f32[4096]{0:T(1024)S(1)}, f32[4096,512]{0,1:T(8,128)S(1)}) fusion(f32[4096,512]{0,1:T(8,128)} %copy-done.1, bf16[4096,512]{1,0:T(8,128)(2,1)} %bitcast.97, bf16[1,512,512]{2,1,0:T(8,128)(2,1)S(1)} %copy-done.4), kind=kOutput, calls=%fused_computation.105 | convolution fusion | flops 2151673856 | bytes 21512192 | tf_op jit(solution)/shard_map/dot_general | solution.py:48
  331.2 15.8 %fusion.94 = (f32[4096]{0:T(1024)S(1)}, f32[4096,512]{0,1:T(8,128)}) fusion(f32[4096,512]{0,1:T(8,128)} %copy-done.2, bf16[1,1024,512]{2,1,0:T(8,128)(2,1)S(1)} %copy-done, f32[512]{0:T(512)S(1)} %bitcast.112, f32[4096]{0:T(1024)S(1)} %add_rsqrt_fusion.1, f32[4096]{0:T(1024)S(1)} %broadcast_multiply_fusion.1, bf16[1,512,1024]{2,1,0:T(8,128)(2,1)S(1)} %copy-done.11), kind=kOutput, calls=%fused_computation.106 | convolution fusion | flops 8640262144 | bytes 18925568 | tf_op jit(solution)/shard_map/dot_general | solution.py:53
  347.0 4.5 %multiply_reduce_fusion.2 = f32[4096]{0:T(1024)S(1)} fusion(f32[4096,512]{0,1:T(8,128)} %get-tuple-element.76, f32[4096]{0:T(1024)S(1)} %broadcast_multiply_fusion), kind=kLoop, calls=%fused_computation.38 | loop fusion | flops 6287360 | bytes 8421376 | tf_op jit(solution)/shard_map/reduce_sum | solution.py:12
  (87 shorter events, 79.7 us)
Async XLA Ops:
  0.0 331.2 %copy-start = (bf16[1,1024,512]{2,1,0:T(8,128)(2,1)S(1)}, bf16[1,1024,512]{2,1,0:T(8,128)(2,1)}, u32[]{:S(2)}) copy-start(bf16[1,1024,512]{2,1,0:T(8,128)(2,1)} %param.20) | copy-start | bytes 3145732
  63.5 7.8 %copy-start.9 = (bf16[512]{0:T(512)(128)(2,1)S(1)}, bf16[512]{0:T(512)(128)(2,1)}, u32[]{:S(2)}) copy-start(bf16[512]{0:T(512)(128)(2,1)} %param.23) | copy-start | bytes 3076
  63.5 8.4 %copy-start.7 = (f32[1,2,512]{2,1,0:T(2,128)S(1)}, f32[1,2,512]{2,1,0:T(2,128)}, u32[]{:S(2)}) copy-start(f32[1,2,512]{2,1,0:T(2,128)} %param.21) | copy-start | bytes 12292
  63.6 71.1 %copy-start.5 = (bf16[128,512]{1,0:T(8,128)(2,1)S(1)}, bf16[128,512]{1,0:T(8,128)(2,1)}, u32[]{:S(2)}) copy-start(bf16[128,512]{1,0:T(8,128)(2,1)} %param.16) | copy-start | bytes 393220
  68.1 51.6 %all-to-all-start.1 = ((bf16[32,256,128]{2,1,0:T(8,128)(2,1)}), bf16[32,256,128]{2,1,0:T(8,128)(2,1)S(1)}, u32[]{:S(2)}, u32[]{:S(2)}) async-start(bf16[32,256,128]{2,1,0:T(8,128)(2,1)} %select_select_fusion), calls=%async_computation.1 | async-start | bytes 4194304 | tf_op jit(solution)/shard_map/all_to_all | solution.py:105
  138.3 3.4 copy-start.1
  139.3 2.6 copy-start.10
  218.0 101.8 %copy-start.4 = (bf16[1,512,512]{2,1,0:T(8,128)(2,1)S(1)}, bf16[1,512,512]{2,1,0:T(8,128)(2,1)}, u32[]{:S(2)}) copy-start(bf16[1,512,512]{2,1,0:T(8,128)(2,1)} %param.18) | copy-start | bytes 1572868
  326.9 3.2 copy-start.2
  326.9 4.2 %copy-start.11 = (bf16[1,512,1024]{2,1,0:T(8,128)(2,1)S(1)}, bf16[1,512,1024]{2,1,0:T(8,128)(2,1)}, u32[]{:S(2)}) copy-start(bf16[1,512,1024]{2,1,0:T(8,128)(2,1)} %param.19) | copy-start | bytes 3145732
  347.0 5.8 %copy-start.3 = (f32[4096,512]{0,1:T(8,128)S(1)}, f32[4096,512]{0,1:T(8,128)}, u32[]{:S(2)}) copy-start(f32[4096,512]{0,1:T(8,128)} %get-tuple-element.76) | copy-start | bytes 25165828
  347.0 5.8 %copy-start.6 = (f32[512]{0:T(512)S(1)}, f32[512]{0:T(512)}, u32[]{:S(2)}) copy-start(f32[512]{0:T(512)} %convert_element_type.67) | copy-start | bytes 6148
  347.0 5.8 %copy-start.8 = (f32[512]{0:T(512)S(1)}, f32[512]{0:T(512)}, u32[]{:S(2)}) copy-start(f32[512]{0:T(512)} %param.22) | copy-start | bytes 6148
where the time goes:
time: 358 us; the launch traced here: 356 us
  local copies, waits for them, and re-layouts  140 us (39%)
  matrix products  133 us (37%)
  waiting for transfers between devices  47.8 us (13%)
  other arithmetic  17.4 us (5%)
  blocking collectives  13.7 us (4%)
    sub x8, matrix products, attend_slate(): probs = jax.nn.softmax(scores, axis=-1).astype(jnp.bfloat16)  57.8 us
    all_to_all x1, waiting for transfers between devices, per_device(): lax.all_to_all(found, ('gx', 'gy'), split_axis=0, concat_axis=0, tiled=True)  47.8 us
    dot_general x8, matrix products, attend_slate(): jnp.einsum('hqk,khd->qhd', probs, values, preferred_element_type=jnp.floa...  35.3 us
    gather x1, local copies, waits for them, and re-layouts, fetch_rows(): rows = jnp.take(item_table, jnp.maximum(flat, 0), axis=0)  31.1 us
    while x3, local copies, waits for them, and re-layouts, score_slates(): lax.map(attend_slate, (query, keys, values)).reshape(slates * length, model)  29.2 us
    dot_general x1, matrix products, score_slates(): jnp.dot(inner, w_down[0], preferred_element_type=jnp.float32)  15.8 us
    scatter x1, local copies, waits for them, and re-layouts, per_device(): jnp.full((shards * capacity,), -1, jnp.int32).at[position].set(row_index)  15.5 us
    gather x1, local copies, waits for them, and re-layouts, per_device(): emb = jnp.take(returned, position, axis=0).reshape(slates, length, width)  14.9 us
  transfers between devices with their start and end apart: 1, of which 1 were waited for; matrix products, arithmetic and copies ran while one was open for 0% of the time, Pallas kernels for 0%

commit v1 on v0

v1 whole, which is shorter than its diff:
```python
import functools

import jax
import jax.numpy as jnp
from jax import lax
from jax.experimental import pallas as pl
from jax.experimental.pallas import tpu as pltpu
from jax.sharding import PartitionSpec as P

HEADS = 8


def dot(a, b):
    return jnp.dot(a, b, preferred_element_type=jnp.float32)


def dot_nt(a, b):
    return lax.dot_general(a, b, (((1,), (1,)), ((), ())), preferred_element_type=jnp.float32)


def layer_norm(values, gain):
    mean = jnp.mean(values, axis=-1, keepdims=True)
    centred = values - mean
    variance = jnp.mean(centred * centred, axis=-1, keepdims=True)
    return centred * lax.rsqrt(variance + 1e-05) * gain


def plan_kernel(owner_ref, row_ref, outgoing_ref, position_ref, *, shards, capacity):
    slates, length = row_ref.shape
    tri = (
        lax.broadcasted_iota(jnp.int32, (length, length), 0)
        <= lax.broadcasted_iota(jnp.int32, (length, length), 1)
    ).astype(jnp.float32).astype(jnp.bfloat16)
    shard_ids = lax.broadcasted_iota(jnp.int32, (shards, length), 0)
    slot_ids = lax.broadcasted_iota(jnp.int32, (capacity, length), 0)
    before = jnp.zeros((shards, 1), jnp.float32)
    acc = jnp.zeros((3 * shards, capacity), jnp.float32)
    for s in range(slates):
        owner = owner_ref[s : s + 1, :]
        row = row_ref[s : s + 1, :]
        onehot = (owner == shard_ids).astype(jnp.float32)
        counts = dot(onehot.astype(jnp.bfloat16), tri) + before
        before = counts[:, length - 1 :]
        slot = (jnp.sum(counts * onehot, axis=0, keepdims=True) - 1.0).astype(jnp.int32)
        position_ref[s : s + 1, :] = owner * capacity + slot
        digits = [(row & 255), ((row >> 8) & 255), (row >> 16)]
        lhs = jnp.concatenate(
            [onehot * digit.astype(jnp.float32) for digit in digits], axis=0
        ).astype(jnp.bfloat16)
        chosen = (slot == slot_ids).astype(jnp.float32).astype(jnp.bfloat16)
        acc = acc + dot_nt(lhs, chosen)
    parts = acc.astype(jnp.int32)
    outgoing_ref[...] = (
        parts[:shards] + (parts[shards : 2 * shards] << 8) + (parts[2 * shards :] << 16)
    )


def plan(owner, row_index, shards, capacity):
    return pl.pallas_call(
        functools.partial(plan_kernel, shards=shards, capacity=capacity),
        out_shape=(
            jax.ShapeDtypeStruct((shards, capacity), jnp.int32),
            jax.ShapeDtypeStruct(row_index.shape, jnp.int32),
        ),
        name="plan",
    )(owner, row_index)


def slate_kernel(
    position_ref,
    rows_ref,
    w_in_ref,
    w_qkv_ref,
    w_out_ref,
    w_up_ref,
    w_down_ref,
    gains_ref,
    final_gain_ref,
    w_score_ref,
    out_ref,
    table_ref,
    emb_ref,
    mixed_ref,
):
    slate = pl.program_id(0)
    length = emb_ref.shape[0]
    model = w_in_ref.shape[1]
    head_dim = model // HEADS
    pair = 2 * head_dim

    @pl.when(slate == 0)
    def _():
        table_ref[...] = rows_ref[...].astype(jnp.float32)

    def pick(group, carry):
        for j in range(16):
            r = group * 16 + j
            p = position_ref[slate * length + r]
            emb_ref[pl.ds(r, 1), :] = table_ref[pl.ds(p, 1), :]
        return carry

    lax.fori_loop(0, length // 16, pick, 0)

    resid = dot(emb_ref[...].astype(jnp.bfloat16), w_in_ref[...])
    normed = layer_norm(resid, gains_ref[0:1, :]).astype(jnp.bfloat16)
    lane = lax.broadcasted_iota(jnp.int32, (1, pair), 1)
    low = lane < head_dim
    scale = head_dim ** (-0.5)
    low_scale = jnp.where(low, scale, 0.0).astype(jnp.bfloat16)
    high_scale = jnp.where(low, 0.0, scale).astype(jnp.bfloat16)
    low_one = jnp.where(low, 1.0, 0.0).astype(jnp.bfloat16)
    high_one = jnp.where(low, 0.0, 1.0).astype(jnp.bfloat16)
    for h in range(HEADS // 2):
        at = h * pair
        query = dot(normed, w_qkv_ref[:, at : at + pair]).astype(jnp.bfloat16)
        keys = dot(normed, w_qkv_ref[:, model + at : model + at + pair]).astype(jnp.bfloat16)
        values = dot(
            normed, w_qkv_ref[:, 2 * model + at : 2 * model + at + pair]
        ).astype(jnp.bfloat16)

        def attend(mask, own, other):
            scores = dot_nt(query * mask, keys)
            top = jnp.max(scores, axis=-1, keepdims=True)
            probs = jnp.exp(scores - top).astype(jnp.bfloat16)
            return dot(probs, values * own + other)

        first = attend(low_scale, low_one, high_one)
        second = attend(high_scale, high_one, low_one)
        total = pltpu.roll(jnp.where(low, second, first), head_dim, 1)
        mixed_ref[:, at : at + pair] = (jnp.where(low, first, second) / total).astype(jnp.bfloat16)
    resid = resid + dot(mixed_ref[...], w_out_ref[...])
    normed = layer_norm(resid, gains_ref[1:2, :]).astype(jnp.bfloat16)
    inner = jax.nn.gelu(dot(normed, w_up_ref[...])).astype(jnp.bfloat16)
    resid = resid + dot(inner, w_down_ref[...])
    final = layer_norm(resid, final_gain_ref[...])
    logits = jnp.sum(final * w_score_ref[...].astype(jnp.float32), axis=-1, keepdims=True)
    logits = jnp.transpose(jnp.broadcast_to(logits, (length, 128)))[0:1, :]
    shifted = logits - jnp.max(logits, axis=-1, keepdims=True)
    out_ref[pl.ds(slate, 1), :] = shifted - jnp.log(
        jnp.sum(jnp.exp(shifted), axis=-1, keepdims=True)
    )


def score_slates(
    position, rows, slates, length, w_in, w_qkv, w_out, w_up, w_down, norm_gains, final_gain, w_score
):
    width, model = w_in.shape
    whole = lambda a: pl.BlockSpec(a.shape, lambda i, *_: (0,) * a.ndim)
    operands = (
        rows,
        w_in,
        w_qkv[0],
        w_out[0],
        w_up[0],
        w_down[0],
        norm_gains[0],
        final_gain[None, :],
        w_score[None, :],
    )
    return pl.pallas_call(
        slate_kernel,
        grid_spec=pltpu.PrefetchScalarGridSpec(
            num_scalar_prefetch=1,
            grid=(slates,),
            in_specs=[whole(a) for a in operands],
            out_specs=pl.BlockSpec((slates, length), lambda i, *_: (0, 0)),
            scratch_shapes=[
                pltpu.VMEM(rows.shape, jnp.float32),
                pltpu.VMEM((length, width), jnp.float32),
                pltpu.VMEM((length, model), jnp.bfloat16),
            ],
        ),
        out_shape=jax.ShapeDtypeStruct((slates, length), jnp.float32),
        compiler_params=pltpu.CompilerParams(
            dimension_semantics=("arbitrary",), vmem_limit_bytes=56 * 1024 * 1024
        ),
        name="slates",
    )(position, *operands)


def per_device(
    candidate_owner,
    candidate_row,
    item_table,
    w_in,
    w_qkv,
    w_out,
    w_up,
    w_down,
    norm_gains,
    final_gain,
    w_score,
):
    slates, length, unused = candidate_owner.shape
    width = item_table.shape[1]
    shards = lax.axis_size(("gx", "gy"))
    capacity = max(2, 2 * slates * length // shards)
    outgoing, position = plan(candidate_owner[:, :, 0], candidate_row, shards, capacity)
    wanted = lax.all_to_all(outgoing, ("gx", "gy"), split_axis=0, concat_axis=0, tiled=True)
    found = item_table.at[wanted.reshape(-1)].get(mode="promise_in_bounds")
    found = found.reshape(shards, capacity, width)
    returned = lax.all_to_all(found, ("gx", "gy"), split_axis=0, concat_axis=0, tiled=True)
    return score_slates(
        position.reshape(-1),
        returned.reshape(shards * capacity, width),
        slates,
        length,
        w_in,
        w_qkv,
        w_out,
        w_up,
        w_down,
        norm_gains,
        final_gain,
        w_score,
    )


def solution(mesh):
    return jax.shard_map(
        per_device,
        mesh=mesh,
        in_specs=(
            P(("gx", "gy"), None, None),
            P(("gx", "gy"), None),
            P(("gx", "gy"), None),
            P(),
            P(),
            P(),
            P(),
            P(),
            P(),
            P(),
            P(),
        ),
        out_specs=P(("gx", "gy"), None),
        check_vma=False,
    )
```

time: 358 us -> 184 us (0.51)
  matrix products: 133 us -> 0 us
  local copies, waits for them, and re-layouts: 140 us -> 41.9 us
  Pallas kernels: 0 us -> 77 us
  other arithmetic: 17.4 us -> 0.04 us
    pallas_call x0 -> x2, Pallas kernels: none -> 77 us  [the longest x1 74 us: score_slates(): pl.pallas_call(slate_kernel, grid_spec=pltpu.PrefetchScalarGridSpec(num_s...]
    dot_general x15 -> x0, matrix products: 75.4 us -> none  [the longest x8 35.3 us: attend_slate(): jnp.einsum('hqk,khd->qhd', probs, values, preferred_element_type=jnp.floa...]
    sub x8 -> x0, matrix products: 57.8 us -> none  [attend_slate(): probs = jax.nn.softmax(scores, axis=-1).astype(jnp.bfloat16)]
    reshape x4 -> x0, local copies, waits for them, and re-layouts: 33.6 us -> none  [the longest x1 11.2 us: score_slates(): query = query.reshape(slates, length, HEADS, head_dim)]
    while x3 -> x0, local copies, waits for them, and re-layouts: 29.2 us -> none  [score_slates(): lax.map(attend_slate, (query, keys, values)).reshape(slates * length, model)]
    scatter x1 -> x0, local copies, waits for them, and re-layouts: 15.5 us -> none  [per_device(): jnp.full((shards * capacity,), -1, jnp.int32).at[position].set(row_index)]
    reduce_sum x6 -> x0, other arithmetic: 8.87 us -> none  [the longest x3 6.53 us: layer_norm(): variance = jnp.mean(centred * centred, axis=-1, keepdims=True)]
    gather x2 -> x1, local copies, waits for them, and re-layouts: 46 us -> 37.3 us  [per_device(): found = item_table.at[wanted.reshape(-1)].get(mode='promise_in_bounds')]
  transfers between devices with their start and end apart: 1 -> 1, of which waited for: 1 -> 1; matrix products, arithmetic and copies ran while one was open for 0% -> 1% of each run, Pallas kernels for 0% -> 0%
where the time goes in v1:
time: 184 us; the launch traced here: 183 us
  Pallas kernels  77 us (42%)
  waiting for transfers between devices  47.2 us (26%)
  local copies, waits for them, and re-layouts  41.9 us (23%)
  blocking collectives  13.6 us (7%)
  starting transfers between devices  3.26 us (2%)
    pallas_call x1, Pallas kernels, score_slates(): pl.pallas_call(slate_kernel, grid_spec=pltpu.PrefetchScalarGridSpec(num_s...  74 us
    all_to_all x1, waiting for transfers between devices, per_device(): lax.all_to_all(found, ('gx', 'gy'), split_axis=0, concat_axis=0, tiled=True)  47.2 us
    gather x1, local copies, waits for them, and re-layouts, per_device(): found = item_table.at[wanted.reshape(-1)].get(mode='promise_in_bounds')  37.3 us
    all_to_all x1, blocking collectives, per_device(): lax.all_to_all(outgoing, ('gx', 'gy'), split_axis=0, concat_axis=0, tiled...  13.6 us
  transfers between devices with their start and end apart: 1, of which 1 were waited for; matrix products, arithmetic and copies ran while one was open for 1% of the time, Pallas kernels for 0%

profile of v1, /device:TPU:1, one launch (start us, length us, event | category | flops | bytes accessed | tf_op | source)
XLA Modules:
  0.0 183.1 jit_solution(13119501576608835229)
XLA Ops:
  0.0 1.3 copy.16
  1.3 3.0 %plan.1 = (s32[32,256]{1,0:T(8,128)}, s32[8,512]{1,0:T(8,128)}) custom-call(s32[8,512]{1,0:T(8,128)} %bitcast.24, s32[8,512]{1,0:T(8,128)} %row_ref.1), custom_call_target="tpu_custom_call" | custom-call | tf_op jit(solution)/shard_map/plan/pallas_call | solution.py:59
  4.4 0.8 copy.12
  5.2 13.6 %all_to_all.14 = s32[32,1,256]{2,1,0:T(1,128)S(1)} all-to-all(s32[32,1,256]{2,1,0:T(1,128)S(1)} %copy.12), channel_id=1, replica_groups=mesh['gx'=8,'gy'=4] {'gx','gy'}, dimensions={0} | all-to-all | bytes 65536 | tf_op jit(solution)/shard_map/all_to_all | solution.py:199
  18.9 37.3 %gather_fusion = bf16[8192,128]{1,0:T(8,128)(2,1)} fusion(bf16[78336,128]{1,0:T(8,128)(2,1)} %param.13, s32[8192]{0:T(1024)S(1)} %broadcast_clamp_fusion), kind=kCustom, calls=%fused_computation | custom fusion | bytes 4227072 | tf_op jit(solution)/shard_map/gather | solution.py:200
  56.1 0.0 copy-start.1
  56.1 0.0 copy-start.2
  56.1 3.3 %all-to-all-start.1 = ((bf16[32,256,128]{2,1,0:T(8,128)(2,1)}), bf16[32,256,128]{2,1,0:T(8,128)(2,1)S(1)}, u32[]{:S(2)}, u32[]{:S(2)}) async-start(bf16[32,256,128]{2,1,0:T(8,128)(2,1)} %bitcast.3), calls=%async_computation.1 | async-start | bytes 4194304 | tf_op jit(solution)/shard_map/all_to_all | solution.py:202
  59.4 0.0 copy-done.1
  59.4 0.6 copy.14
  60.0 0.0 copy-done.2
  60.0 0.6 broadcast_in_dim.8.w_score_ref
  60.6 47.2 %all-to-all-done.1 = bf16[32,256,128]{2,1,0:T(8,128)(2,1)S(1)} async-done(((bf16[32,256,128]{2,1,0:T(8,128)(2,1)}), bf16[32,256,128]{2,1,0:T(8,128)(2,1)S(1)}, u32[]{:S(2)}, u32[]{:S(2)}) %all-to-all-start.1) | async-done | bytes 2097184 | tf_op jit(solution)/shard_map/all_to_all | solution.py:202
  107.8 0.0 copy-start
  107.8 1.3 copy-done
  109.2 74.0 %slates.1 = f32[8,512]{1,0:T(8,128)} custom-call(s32[4096]{0:T(1024)} %bitcast.23, bf16[8192,128]{1,0:T(8,128)(2,1)} %bitcast.16, bf16[128,512]{1,0:T(8,128)(2,1)} %w_in_ref.1, bf16[512,1536]{1,0:T(8,128)(2,1)} %bitcast.17, bf16[512,512]{1,0:T(8,128)(2,1)} %bitcast.20, bf16[512,1024]{1,0:T(8,128)(2,1)} %bitcast.18, bf16[1024,512]{1,0:T(8,128)(2,1)} %bitcast.19, ...), custom_call_target="tpu_custom_call" | custom-call | tf_op jit(solution)/shard_map/slates/pallas_call | solution.py:160
  (2 shorter events, 0.0 us)
Async XLA Ops:
  56.1 3.3 %copy-start.1 = (s32[8,512]{1,0:T(8,128)S(1)}, s32[8,512]{1,0:T(8,128)}, u32[]{:S(2)}) copy-start(s32[8,512]{1,0:T(8,128)} %get-tuple-element.7) | copy-start | bytes 49156
  56.1 3.9 %copy-start.2 = (bf16[512]{0:T(512)(128)(2,1)S(1)}, bf16[512]{0:T(512)(128)(2,1)}, u32[]{:S(2)}) copy-start(bf16[512]{0:T(512)(128)(2,1)} %param.21) | copy-start | bytes 3076
  56.1 51.7 %all-to-all-start.1 = ((bf16[32,256,128]{2,1,0:T(8,128)(2,1)}), bf16[32,256,128]{2,1,0:T(8,128)(2,1)S(1)}, u32[]{:S(2)}, u32[]{:S(2)}) async-start(bf16[32,256,128]{2,1,0:T(8,128)(2,1)} %bitcast.3), calls=%async_computation.1 | async-start | bytes 4194304 | tf_op jit(solution)/shard_map/all_to_all | solution.py:202
  107.8 1.3 copy-start

commit v2 on v1

--- a/solution.py
+++ b/solution.py
@@ -25,8 +25,17 @@
     return centred * lax.rsqrt(variance + 1e-05) * gain
 
 
-def plan_kernel(owner_ref, row_ref, outgoing_ref, position_ref, *, shards, capacity):
+def cuts(total, parts):
+    return [total * part // 8 for part in parts]
+
+
+SLOT_PARTS = (0, 4, 8)
+SLATE_PARTS = (0, 3, 8)
+
+
+def plan_kernel(owner_ref, row_ref, outgoing_ref, position_ref, stage_ref, *, slot_cuts, slate_cuts):
     slates, length = row_ref.shape
+    shards, unused, capacity = outgoing_ref.shape
     tri = (
         lax.broadcasted_iota(jnp.int32, (length, length), 0)
         <= lax.broadcasted_iota(jnp.int32, (length, length), 1)
@@ -36,13 +45,24 @@
     before = jnp.zeros((shards, 1), jnp.float32)
     acc = jnp.zeros((3 * shards, capacity), jnp.float32)
     for s in range(slates):
-        owner = owner_ref[s : s + 1, :]
+        owner = owner_ref[s]
         row = row_ref[s : s + 1, :]
         onehot = (owner == shard_ids).astype(jnp.float32)
         counts = dot(onehot.astype(jnp.bfloat16), tri) + before
         before = counts[:, length - 1 :]
         slot = (jnp.sum(counts * onehot, axis=0, keepdims=True) - 1.0).astype(jnp.int32)
-        position_ref[s : s + 1, :] = owner * capacity + slot
+        position = owner * slot_cuts[1] + slot
+        for c in range(1, len(slot_cuts) - 1):
+            low, high = slot_cuts[c], slot_cuts[c + 1]
+            later = shards * low + owner * (high - low) + slot - low
+            position = jnp.where(slot >= low, later, position)
+        position_ref[s : s + 1, :] = position
+        largest = jnp.max(slot, axis=-1, keepdims=True)
+        stage = jnp.zeros((1, 128), jnp.int32)
+        for c in range(1, len(slot_cuts) - 1):
+            late = (largest >= slot_cuts[c]) | (s >= slate_cuts[c])
+            stage = jnp.where(late, c, stage)
+        stage_ref[s : s + 1, :] = stage
         digits = [(row & 255), ((row >> 8) & 255), (row >> 16)]
         lhs = jnp.concatenate(
             [onehot * digit.astype(jnp.float32) for digit in digits], axis=0
@@ -50,25 +70,49 @@
         chosen = (slot == slot_ids).astype(jnp.float32).astype(jnp.bfloat16)
         acc = acc + dot_nt(lhs, chosen)
     parts = acc.astype(jnp.int32)
-    outgoing_ref[...] = (
+    outgoing_ref[:, 0, :] = (
         parts[:shards] + (parts[shards : 2 * shards] << 8) + (parts[2 * shards :] << 16)
     )
 
 
-def plan(owner, row_index, shards, capacity):
+def plan(owner, row_index, shards, slot_cuts, slate_cuts):
+    slates = row_index.shape[0]
     return pl.pallas_call(
-        functools.partial(plan_kernel, shards=shards, capacity=capacity),
+        functools.partial(plan_kernel, slot_cuts=slot_cuts, slate_cuts=slate_cuts),
         out_shape=(
-            jax.ShapeDtypeStruct((shards, capacity), jnp.int32),
+            jax.ShapeDtypeStruct((shards, 1, slot_cuts[-1]), jnp.int32),
             jax.ShapeDtypeStruct(row_index.shape, jnp.int32),
+            jax.ShapeDtypeStruct((slates, 128), jnp.int32),
         ),
         name="plan",
     )(owner, row_index)
 
 
-def slate_kernel(
+def stage_kernel(position_ref, stage_ref, *refs, number):
+    row_refs, refs = refs[: number + 1], refs[number + 1 :]
+    if number:
+        done_ref, refs = refs[0], refs[1:]
+        refs[-4][...] = done_ref[...]
+    table_ref = refs[-3]
+    start = 0
+    for rows_ref in row_refs:
+        count = rows_ref.shape[0]
+        table_ref[start : start + count, :] = rows_ref[...].astype(jnp.float32)
+        start += count
+
+    def step(slate, carry):
+        @pl.when(stage_ref[slate, 0] == number)
+        def _():
+            one_slate(slate, position_ref, *refs)
+
+        return carry
+
+    lax.fori_loop(0, stage_ref.shape[0], step, 0)
+
+
+def one_slate(
+    slate,
     position_ref,
-    rows_ref,
     w_in_ref,
     w_qkv_ref,
     w_out_ref,
@@ -82,20 +126,15 @@
     emb_ref,
     mixed_ref,
 ):
-    slate = pl.program_id(0)
     length = emb_ref.shape[0]
     model = w_in_ref.shape[1]
     head_dim = model // HEADS
     pair = 2 * head_dim
 
-    @pl.when(slate == 0)
-    def _():
-        table_ref[...] = rows_ref[...].astype(jnp.float32)
-
     def pick(group, carry):
         for j in range(16):
             r = group * 16 + j
-            p = position_ref[slate * length + r]
+            p = position_ref[slate, r]
             emb_ref[pl.ds(r, 1), :] = table_ref[pl.ds(p, 1), :]
         return carry
 
@@ -141,41 +180,34 @@
     )
 
 
-def score_slates(
-    position, rows, slates, length, w_in, w_qkv, w_out, w_up, w_down, norm_gains, final_gain, w_score
-):
+def run_stage(number, position, stage, rows, done, weights, share):
+    slates, length = position.shape
+    w_in, w_qkv, w_out, w_up, w_down = weights[:5]
     width, model = w_in.shape
-    whole = lambda a: pl.BlockSpec(a.shape, lambda i, *_: (0,) * a.ndim)
-    operands = (
-        rows,
-        w_in,
-        w_qkv[0],
-        w_out[0],
-        w_up[0],
-        w_down[0],
-        norm_gains[0],
-        final_gain[None, :],
-        w_score[None, :],
-    )
+    total = sum(r.shape[0] for r in rows)
+    smem = pl.BlockSpec(memory_space=pltpu.SMEM)
+    vmem = pl.BlockSpec(memory_space=pltpu.VMEM)
+    operands = (*rows, *([done] if number else []), *weights)
+    matmuls = sum(w.size for w in (w_in, w_qkv, w_out, w_up, w_down))
+    flops = 2 * length * (matmuls + 2 * length * model)
     return pl.pallas_call(
-        slate_kernel,
-        grid_spec=pltpu.PrefetchScalarGridSpec(
-            num_scalar_prefetch=1,
-            grid=(slates,),
-            in_specs=[whole(a) for a in operands],
-            out_specs=pl.BlockSpec((slates, length), lambda i, *_: (0, 0)),
-            scratch_shapes=[
-                pltpu.VMEM(rows.shape, jnp.float32),
-                pltpu.VMEM((length, width), jnp.float32),
-                pltpu.VMEM((length, model), jnp.bfloat16),
-            ],
+        functools.partial(stage_kernel, number=number),
+        in_specs=[smem, smem] + [vmem] * len(operands),
+        out_specs=vmem,
+        scratch_shapes=[
+            pltpu.VMEM((total, width), jnp.float32),
+            pltpu.VMEM((length, width), jnp.float32),
+            pltpu.VMEM((length, model), jnp.bfloat16),
+        ],
+        out_shape=jax.ShapeDtypeStruct((slates, length), jnp.float32),
+        compiler_params=pltpu.CompilerParams(vmem_limit_bytes=56 * 1024 * 1024),
+        cost_estimate=pl.CostEstimate(
+            flops=share * flops,
+            transcendentals=share * HEADS * length * length,
+            bytes_accessed=2 * matmuls,
         ),
-        out_shape=jax.ShapeDtypeStruct((slates, length), jnp.float32),
-        compiler_params=pltpu.CompilerParams(
-            dimension_semantics=("arbitrary",), vmem_limit_bytes=56 * 1024 * 1024
-        ),
-        name="slates",
-    )(position, *operands)
+        name="stage" + str(number),
+    )(position, stage, *operands)
 
 
 def per_device(
@@ -195,25 +227,33 @@
     width = item_table.shape[1]
     shards = lax.axis_size(("gx", "gy"))
     capacity = max(2, 2 * slates * length // shards)
-    outgoing, position = plan(candidate_owner[:, :, 0], candidate_row, shards, capacity)
+    slot_cuts = cuts(capacity, SLOT_PARTS)
+    slate_cuts = cuts(slates, SLATE_PARTS)
+    owner = candidate_owner.reshape(slates, 1, length)
+    outgoing, position, stage = plan(owner, candidate_row, shards, slot_cuts, slate_cuts)
     wanted = lax.all_to_all(outgoing, ("gx", "gy"), split_axis=0, concat_axis=0, tiled=True)
-    found = item_table.at[wanted.reshape(-1)].get(mode="promise_in_bounds")
-    found = found.reshape(shards, capacity, width)
-    returned = lax.all_to_all(found, ("gx", "gy"), split_axis=0, concat_axis=0, tiled=True)
-    return score_slates(
-        position.reshape(-1),
-        returned.reshape(shards * capacity, width),
-        slates,
-        length,
+    wanted = wanted.reshape(shards, capacity)
+    weights = (
         w_in,
-        w_qkv,
-        w_out,
-        w_up,
-        w_down,
-        norm_gains,
-        final_gain,
-        w_score,
-    )
+        w_qkv[0],
+        w_out[0],
+        w_up[0],
+        w_down[0],
+        norm_gains[0],
+        final_gain[None, :],
+        w_score[None, :],
+    )
+    rows, scores = [], None
+    for c in range(len(slot_cuts) - 1):
+        size = slot_cuts[c + 1] - slot_cuts[c]
+        index = wanted[:, slot_cuts[c] : slot_cuts[c + 1]].reshape(-1)
+        found = item_table.at[index].get(mode="promise_in_bounds").reshape(shards, size, width)
+        moved = lax.all_to_all(found, ("gx", "gy"), split_axis=0, concat_axis=0, tiled=True)
+        rows.append(moved.reshape(shards * size, width))
+    for c in range(len(rows)):
+        share = slate_cuts[c + 1] - slate_cuts[c]
+        scores = run_stage(c, position, stage, rows[: c + 1], scores, weights, share)
+    return scores
 
 
 def solution(mesh):

time: 184 us -> 158 us (0.86)
  waiting for transfers between devices: 47.2 us -> 2.83 us
  Pallas kernels: 77 us -> 85.3 us
  local copies, waits for them, and re-layouts: 41.9 us -> 48.8 us
  starting transfers between devices: 3.26 us -> 6.22 us
    all_to_all x1 -> x2, waiting for transfers between devices: 47.2 us -> 2.83 us  [per_device(): lax.all_to_all(found, ('gx', 'gy'), split_axis=0, concat_axis=0, tiled=True)]
    gather x1 -> x2, local copies, waits for them, and re-layouts: 37.3 us -> 47.2 us  [per_device(): item_table.at[index].get(mode='promise_in_bounds')]
    pallas_call x2 -> x3, Pallas kernels: 77 us -> 85.3 us  [the longest x2 82.2 us: run_stage(): pl.pallas_call(functools.partial(stage_kernel, number=number), in_specs=[...]
    all_to_all x1 -> x2, starting transfers between devices: 3.26 us -> 6.22 us  [per_device(): lax.all_to_all(found, ('gx', 'gy'), split_axis=0, concat_axis=0, tiled=True)]
    unnamed x8 -> x7, local copies, waits for them, and re-layouts: 3.27 us -> 1.03 us
  transfers between devices with their start and end apart: 1 -> 2, of which waited for: 1 -> 1; matrix products, arithmetic and copies ran while one was open for 1% -> 15% of each run, Pallas kernels for 0% -> 20%
where the time goes in v2:
time: 158 us; the launch traced here: 157 us
  Pallas kernels  85.3 us (54%)
  local copies, waits for them, and re-layouts  48.8 us (31%)
  blocking collectives  13.8 us (9%)
  starting transfers between devices  6.22 us (4%)
  waiting for transfers between devices  2.83 us (2%)
    pallas_call x2, Pallas kernels, run_stage(): pl.pallas_call(functools.partial(stage_kernel, number=number), in_specs=[...  82.2 us
    gather x2, local copies, waits for them, and re-layouts, per_device(): item_table.at[index].get(mode='promise_in_bounds')  47.2 us
    all_to_all x1, blocking collectives, per_device(): lax.all_to_all(outgoing, ('gx', 'gy'), split_axis=0, concat_axis=0, tiled...  13.8 us
    all_to_all x2, starting transfers between devices, per_device(): lax.all_to_all(found, ('gx', 'gy'), split_axis=0, concat_axis=0, tiled=True)  6.22 us
  transfers between devices with their start and end apart: 2, of which 1 were waited for; matrix products, arithmetic and copies ran while one was open for 15% of the time, Pallas kernels for 20%

profile of v2, /device:TPU:1, one launch (start us, length us, event | category | flops | bytes accessed | tf_op | source)
XLA Modules:
  0.0 157.1 jit_solution(5002638628877801494)
XLA Ops:
  0.0 0.0 copy-start.2
  0.0 3.1 %plan.1 = (s32[32,1,256]{2,1,0:T(1,128)}, s32[8,512]{1,0:T(8,128)}, s32[8,128]{1,0:T(8,128)}) custom-call(s32[8,1,512]{2,1,0:T(1,128)} %bitcast.26, s32[8,512]{1,0:T(8,128)} %row_ref.1), custom_call_target="tpu_custom_call" | custom-call | tf_op jit(solution)/shard_map/plan/pallas_call | solution.py:80
  3.1 13.8 %all_to_all.15 = s32[32,1,256]{2,1,0:T(1,128)S(1)} all-to-all(s32[32,1,256]{2,1,0:T(1,128)} %get-tuple-element.10), channel_id=1, replica_groups=mesh['gx'=8,'gy'=4] {'gx','gy'}, dimensions={0} | all-to-all | bytes 65536 | tf_op jit(solution)/shard_map/all_to_all | solution.py:234
  16.9 23.6 %gather_fusion = bf16[4096,128]{1,0:T(8,128)(2,1)} fusion(bf16[78336,128]{1,0:T(8,128)(2,1)} %param.13, s32[4096]{0:T(1024)S(1)} %broadcast_clamp_fusion.1), kind=kCustom, calls=%fused_computation | custom fusion | bytes 2113536 | tf_op jit(solution)/shard_map/gather | solution.py:250
  40.6 3.0 %all-to-all-start.1 = ((bf16[32,128,128]{2,1,0:T(8,128)(2,1)}), bf16[32,128,128]{2,1,0:T(8,128)(2,1)S(1)}, u32[]{:S(2)}, u32[]{:S(2)}) async-start(bf16[32,128,128]{2,1,0:T(8,128)(2,1)} %bitcast.3), calls=%async_computation.1 | async-start | bytes 2097152 | tf_op jit(solution)/shard_map/all_to_all | solution.py:251
  43.7 23.6 %gather_fusion.1 = bf16[4096,128]{1,0:T(8,128)(2,1)} fusion(bf16[78336,128]{1,0:T(8,128)(2,1)} %param.13, s32[4096]{0:T(1024)S(1)} %broadcast_clamp_fusion), kind=kCustom, calls=%fused_computation.1 | custom fusion | bytes 2113536 | tf_op jit(solution)/shard_map/gather | solution.py:250
  67.3 2.8 %all-to-all-done.1 = bf16[32,128,128]{2,1,0:T(8,128)(2,1)S(1)} async-done(((bf16[32,128,128]{2,1,0:T(8,128)(2,1)}), bf16[32,128,128]{2,1,0:T(8,128)(2,1)S(1)}, u32[]{:S(2)}, u32[]{:S(2)}) %all-to-all-start.1) | async-done | bytes 1048608 | tf_op jit(solution)/shard_map/all_to_all | solution.py:251
  70.1 0.0 copy-start
  70.1 3.2 %all-to-all-start.2 = ((bf16[32,128,128]{2,1,0:T(8,128)(2,1)}), bf16[32,128,128]{2,1,0:T(8,128)(2,1)S(1)}, u32[]{:S(2)}, u32[]{:S(2)}) async-start(bf16[32,128,128]{2,1,0:T(8,128)(2,1)} %bitcast.7), calls=%async_computation.2 | async-start | bytes 2097152 | tf_op jit(solution)/shard_map/all_to_all | solution.py:251
  73.3 0.0 copy-done.2
  73.3 0.6 broadcast_in_dim.9.refs_8_.refs_10_
  73.9 0.0 copy-done
  73.9 31.4 %stage0.1.refs_2_ = f32[8,512]{1,0:T(8,128)} custom-call(s32[8,512]{1,0:T(8,128)} %get-tuple-element.8.position_ref, s32[8,128]{1,0:T(8,128)} %get-tuple-element.9.stage_ref, bf16[4096,128]{1,0:T(8,128)(2,1)} %bitcast.18, bf16[128,512]{1,0:T(8,128)(2,1)} %refs_3_.1, bf16[512,1536]{1,0:T(8,128)(2,1)} %bitcast.27, bf16[512,512]{1,0:T(8,128)(2,1)} %bitcast.33, ...), custom_call_target="tpu_custom_call" | custom-call | flops 8254390272 | bytes 4325376 | tf_op jit(solution)/shard_map/stage0/pallas_call | solution.py:193
  105.3 0.0 all-to-all-done.2
  105.3 0.0 copy-start.1
  105.3 1.0 copy-done.1
  106.3 50.8 %stage1.1 = f32[8,512]{1,0:T(8,128)} custom-call(s32[8,512]{1,0:T(8,128)} %get-tuple-element.8.position_ref, s32[8,128]{1,0:T(8,128)} %get-tuple-element.9.stage_ref, bf16[4096,128]{1,0:T(8,128)(2,1)} %bitcast.19, bf16[4096,128]{1,0:T(8,128)(2,1)} %bitcast.20, f32[8,512]{1,0:T(8,128)} %stage0.1.refs_2_, bf16[128,512]{1,0:T(8,128)(2,1)} %refs_3_.1, ...), custom_call_target="tpu_custom_call" | custom-call | flops 13757317120 | bytes 4325376 | tf_op jit(solution)/shard_map/stage1/pallas_call | solution.py:193
  (6 shorter events, 0.1 us)
Async XLA Ops:
  0.0 73.3 %copy-start.2 = (bf16[512]{0:T(512)(128)(2,1)S(1)}, bf16[512]{0:T(512)(128)(2,1)}, u32[]{:S(2)}) copy-start(bf16[512]{0:T(512)(128)(2,1)} %param.21) | copy-start | bytes 3076
  40.6 29.5 %all-to-all-start.1 = ((bf16[32,128,128]{2,1,0:T(8,128)(2,1)}), bf16[32,128,128]{2,1,0:T(8,128)(2,1)S(1)}, u32[]{:S(2)}, u32[]{:S(2)}) async-start(bf16[32,128,128]{2,1,0:T(8,128)(2,1)} %bitcast.3), calls=%async_computation.1 | async-start | bytes 2097152 | tf_op jit(solution)/shard_map/all_to_all | solution.py:251
  70.1 3.8 %copy-start = (bf16[32,128,128]{2,1,0:T(8,128)(2,1)}, bf16[32,128,128]{2,1,0:T(8,128)(2,1)S(1)}, u32[]{:S(2)}) copy-start(bf16[32,128,128]{2,1,0:T(8,128)(2,1)S(1)} %all-to-all-done.1) | copy-start | bytes 3145732
  70.1 35.2 %all-to-all-start.2 = ((bf16[32,128,128]{2,1,0:T(8,128)(2,1)}), bf16[32,128,128]{2,1,0:T(8,128)(2,1)S(1)}, u32[]{:S(2)}, u32[]{:S(2)}) async-start(bf16[32,128,128]{2,1,0:T(8,128)(2,1)} %bitcast.7), calls=%async_computation.2 | async-start | bytes 2097152 | tf_op jit(solution)/shard_map/all_to_all | solution.py:251
  105.3 1.0 copy-start.1
